TPU v7x, 768 devices: a whole 4x8x12 slice. The times are simulated.
768 devices in a mesh: blk: 16 (over x_lo, y), fsdp: 48 (over z, x_hi, core).
Axes of the slice: x: 4 (x_hi: 2, x_lo: 2; x = x_hi * 2 + x_lo), y: 8, z: 12, core: 2. Of those that a mesh axis runs over, the one named last changes fastest.
Arguments:
- tokens: bfloat16 [16, 6144, 2304], P('blk', 'fsdp'), may hold values from -6 to 6
- cotangent: bfloat16 [16, 6144, 512], P('blk', 'fsdp'), may hold values from -6 to 6
- weights: float32 [16, 2304, 512], P('blk', 'fsdp'), may hold values from -6 to 6
- moment_one: float32 [16, 2304, 512], P('blk', 'fsdp'), may hold values from -6 to 6
- moment_two: float32 [16, 2304, 512], P('blk', 'fsdp'), may hold values from 1 to 16
- gossip: int32 [16, 3], P('blk'), may hold values from 1 to 8
Outputs:
- key_out: bfloat16 [16, 6144, 512], P('blk', 'fsdp')
- input_grad: bfloat16 [16, 6144, 2304], P('blk', 'fsdp')
- weights_out: float32 [16, 2304, 512], P('blk', 'fsdp')
- moment_one_out: float32 [16, 2304, 512], P('blk', 'fsdp')
- moment_two_out: float32 [16, 2304, 512], P('blk', 'fsdp')
Inputs may be any that keep to these rules, and one draw needn't show every extreme that they name: `gossip`: row r holds the weights given to replica r - 1, to replica r itself and to replica r + 1 on the closed cycle of 16 replicas.
All inputs are finite; a program needn't handle non-finite values.
Results may differ from a plain program's by a relative error of at most 0.005.
Values may be sent and summed in bfloat16 or wider, within the bound.
No kernel may reach another device: no remote copies, remote signals or barrier semaphores. Data moves between devices by JAX's collectives and lax.ppermute only.
A program may use at most 32 MiB of HBM per device.

v0:
```python
import math

import jax
import jax.numpy as jnp
from jax import lax
from jax.sharding import Mesh
from jax.sharding import PartitionSpec as P

FSDP = ("fsdp_0", "fsdp_1", "fsdp_2")


beta_one = 0.9
beta_two = 0.95
learn_rate = 0.05
weight_decay = 0.1
epsilon = 1e-08
correct_one = 1.0 - beta_one**5
correct_two = 1.0 - beta_two**5


def own_block(blocks, axes, turns):
    shape = [lax.axis_size(a) for a in axes]
    blocks = blocks.reshape(*shape, *blocks.shape[1:])
    blocks = blocks.transpose(*turns, *range(len(axes), blocks.ndim))
    blocks = blocks.reshape(-1, *blocks.shape[len(axes) :])
    for k in turns:
        blocks = lax.psum_scatter(blocks, axes[k], scatter_dimension=0, tiled=True)
    return blocks[0]


def split_up(shard, dim, length):
    before, after = (shard.shape[:dim], shard.shape[dim + 1 :])
    return jnp.moveaxis(shard.reshape(*before, length, -1, *after), dim, 0)


def scatter_axes(shard, axes, turns, dim):
    length = lax.axis_size(axes)
    return own_block(split_up(shard, dim, length), axes, turns)


def from_behind(shard, axis, by):
    length = lax.axis_size(axis)
    return lax.ppermute(shard, axis, [(i, (i + by) % length) for i in range(length)])


def local(tokens, cotangent, weights, moment_one, moment_two, gossip):
    activations = tokens[0]
    upstream = cotangent[0]
    factor = 1.0 / math.sqrt(activations.shape[1])
    compute_weights = weights[0].astype(jnp.bfloat16)
    gathered = lax.all_gather(compute_weights, FSDP, axis=0, tiled=True)
    key_sum = jnp.dot(activations, gathered, preferred_element_type=jnp.float32)
    key_out = (key_sum * factor).astype(jnp.bfloat16)
    product = lax.dot_general(
        upstream, gathered, (((1,), (1,)), ((), ())), preferred_element_type=jnp.float32
    )
    input_grad = (product * factor).astype(jnp.bfloat16)
    product = lax.dot_general(
        activations, upstream, (((0,), (0,)), ((), ())), preferred_element_type=jnp.float32
    )
    gradient = scatter_axes(product * factor, FSDP, (2, 0, 1), 0)
    master = weights[0]
    moment_one_out = beta_one * moment_one[0] + (1.0 - beta_one) * gradient
    moment_two_out = beta_two * moment_two[0] + (1.0 - beta_two) * gradient * gradient
    update = moment_one_out / correct_one / (jnp.sqrt(moment_two_out / correct_two) + epsilon)
    stepped = master - learn_rate * (update + weight_decay * master)
    left_side = from_behind(stepped.astype(jnp.bfloat16), "blk", 1).astype(stepped.dtype)
    right_side = from_behind(stepped.astype(jnp.bfloat16), "blk", -1).astype(stepped.dtype)
    mix_weights = gossip[0].astype(jnp.float32)
    averaged = (
        mix_weights[0] * left_side + mix_weights[1] * stepped + mix_weights[2] * right_side
    ) / (mix_weights[0] + mix_weights[1] + mix_weights[2])
    averaged, moment_one_out, moment_two_out = (averaged, moment_one_out, moment_two_out)
    return (
        key_out[None],
        input_grad[None],
        averaged[None],
        moment_one_out[None],
        moment_two_out[None],
    )


def solution(mesh):
    split = Mesh(
        mesh.devices.reshape(mesh.shape["blk"], 12, 2, 2), ("blk", "fsdp_0", "fsdp_1", "fsdp_2")
    )
    return jax.shard_map(
        local,
        mesh=split,
        in_specs=(
            P("blk", FSDP, None),
            P("blk", FSDP, None),
            P("blk", FSDP, None),
            P("blk", FSDP, None),
            P("blk", FSDP, None),
            P("blk", None),
        ),
        out_specs=(
            P("blk", FSDP, None),
            P("blk", FSDP, None),
            P("blk", FSDP, None),
            P("blk", FSDP, None),
            P("blk", FSDP, None),
        ),
        check_vma=False,
    )
```

profile of v0, /device:TPU:24, one launch (start us, length us, event | category | flops | bytes accessed | tf_op | source)
XLA Modules:
  0.0 200.1 jit_solution(1467541856597344097)
XLA Ops:
  8.0 0.0 reduce-scatter.4.cloned.1.call-start
  8.1 1.0 copy-done
  9.1 1.7 convolution_multiply_fusion
  10.8 3.0 %copy.11 = f32[2,12,2,48,512]{4,3,2,1,0:T(8,128)} copy(f32[2,12,2,48,512]{4,3,0,2,1:T(8,128)S(1)} %bitcast.57) | data formatting | bytes 9437184 | tf_op jit(solution)/shard_map/transpose | solution.py:24
  13.8 0.0 reduce-scatter.4.cloned.1.call-update
  13.9 0.0 reduce-scatter.6.cloned.1.call-start
  13.9 30.1 %reduce-scatter.4.cloned.1.call-done = f32[24,48,512]{2,1,0:T(8,128)} async-done(((f32[48,48,512]{2,1,0:T(8,128)}), f32[24,48,512]{2,1,0:T(8,128)}) %reduce-scatter.4.cloned.1.call-update) | async-done | bytes 2359312 | tf_op jit(solution)/shard_map/reduce_scatter | solution.py:27
  44.0 0.0 reduce-scatter.6.cloned.1.call-update
  44.0 0.0 all-gather.2.cloned.1.call-start
  44.0 0.6 bitcast_convert_fusion
  44.7 0.0 all-gather.2.cloned.1.call-update
  44.7 0.0 reduce-scatter.8.cloned.1.call-start
  44.8 0.6 fusion.18
  47.2 64.3 %reduce-scatter.6.cloned.1.call-done = f32[2,48,512]{2,1,0:T(8,128)} async-done(((f32[24,48,512]{2,1,0:T(8,128)}), f32[2,48,512]{2,1,0:T(8,128)}) %reduce-scatter.6.cloned.1.call-update) | async-done | bytes 196624 | tf_op jit(solution)/shard_map/reduce_scatter | solution.py:27
  111.5 0.0 reduce-scatter.8.cloned.1.call-update
  111.6 61.5 %all-gather.2.cloned.1.call-done = bf16[2304,512]{1,0:T(8,128)(2,1)} async-done(((bf16[48,512]{1,0:T(8,128)(2,1)}), bf16[2304,512]{1,0:T(8,128)(2,1)}) %all-gather.2.cloned.1.call-update) | async-done | bytes 2359312 | tf_op jit(solution)/shard_map/all_gather | solution.py:51
  173.1 3.5 %fusion.1 = bf16[1,128,2304]{2,1,0:T(8,128)(2,1)} fusion(bf16[2304,512]{1,0:T(8,128)(2,1)} %all-gather.2.cloned.1.call-done, bf16[1,128,512]{2,1,0:T(8,128)(2,1)S(1)} %copy-done.2), kind=kOutput, calls=%fused_computation.3 | convolution fusion | flops 302579712 | bytes 3080192 | tf_op jit(solution)/shard_map/dot_general | solution.py:54
  176.6 1.1 fusion.3
  177.7 1.0 fusion.17
  178.7 4.6 %collective-permute-start = (bf16[48,512]{1,0:T(8,128)(2,1)S(1)}, bf16[48,512]{1,0:T(8,128)(2,1)S(1)}, u32[]{:S(2)}, u32[]{:S(2)}) collective-permute-start(bf16[48,512]{1,0:T(8,128)(2,1)S(1)} %get-tuple-element.5), channel_id=1, source_target_pairs={{0,48},{48,96},{96,144},{144,192},{192,240},{240,288},{288,336},{3... | collective-permute-start | bytes 147464 | tf_op jit(solution)/shard_map/ppermute | solution.py:43
  183.3 1.9 collective-permute-start.1
  185.2 1.6 fusion.14
  186.8 3.7 %collective-permute-done.1 = bf16[48,512]{1,0:T(8,128)(2,1)S(1)} collective-permute-done((bf16[48,512]{1,0:T(8,128)(2,1)S(1)}, bf16[48,512]{1,0:T(8,128)(2,1)S(1)}, u32[]{:S(2)}, u32[]{:S(2)}) %collective-permute-start.1) | collective-permute-done | bytes 49184 | tf_op jit(solution)/shard_map/ppermute | solution.py:43
  190.5 2.5 %divide_bitcast_fusion = f32[1,48,512]{2,1,0:T(8,128)} fusion(bf16[48,512]{1,0:T(8,128)(2,1)S(1)} %collective-permute-done.1, f32[48,512]{1,0:T(8,128)S(1)} %get-tuple-element.6, bf16[48,512]{1,0:T(8,128)(2,1)S(1)} %collective-permute-done, f32[]{:T(128)S(6)} %add.47, f32[]{:T(128)} %bitcast.13, f32[]{:T(128)} %bitcast.12, f32[]{:T(128)} %bitcast.5), kind=kLoop, calls=%fused_computation.27 | loop fusion | flops 196608 | bytes 294928 | tf_op jit(solution)/shard_map/broadcast_in_dim | solution.py:77
  (16 shorter events, 0.1 us)
Async XLA Ops:
  8.0 1.1 copy-start
  8.0 36.0 %reduce-scatter.4.cloned.1.call-start = ((), (), s32[]{:S(2)}) async-start(), calls=%async_computation.4 | async-start | bytes 7077888 | tf_op jit(solution)/shard_map/reduce_scatter | solution.py:27
  13.8 30.2 %copy-start.3 = (f32[1,48,512]{2,1,0:T(8,128)S(1)}, f32[1,48,512]{2,1,0:T(8,128)}, u32[]{:S(2)}) copy-start(f32[1,48,512]{2,1,0:T(8,128)} %param.8) | copy-start | bytes 294916
  13.8 30.9 %copy-start.6 = (s32[1,3]{1,0:T(1,128)S(1)}, s32[1,3]{1,0:T(1,128)}, u32[]{:S(2)}) copy-start(s32[1,3]{1,0:T(1,128)} %param.11) | copy-start | bytes 40
  13.8 159.2 %copy-start.2 = (bf16[1,128,512]{2,1,0:T(8,128)(2,1)S(1)}, bf16[1,128,512]{2,1,0:T(8,128)(2,1)}, u32[]{:S(2)}) copy-start(bf16[1,128,512]{2,1,0:T(8,128)(2,1)} %param.7) | copy-start | bytes 393220
  13.9 97.7 %reduce-scatter.6.cloned.1.call-start = ((), (), s32[]{:S(2)}) async-start(), calls=%async_computation.5 | async-start | bytes 2555904 | tf_op jit(solution)/shard_map/reduce_scatter | solution.py:27
  44.0 129.1 %all-gather.2.cloned.1.call-start = ((), (), s32[]{:S(2)}) async-start(), calls=%async_computation.3 | async-start | bytes 2408448 | tf_op jit(solution)/shard_map/all_gather | solution.py:51
  44.7 133.0 %reduce-scatter.8.cloned.1.call-start = ((), (), s32[]{:S(2)}) async-start(), calls=%async_computation.6 | async-start | bytes 294912 | tf_op jit(solution)/shard_map/reduce_scatter | solution.py:27
  111.5 66.2 %copy-start.4 = (f32[1,48,512]{2,1,0:T(8,128)S(1)}, f32[1,48,512]{2,1,0:T(8,128)}, u32[]{:S(2)}) copy-start(f32[1,48,512]{2,1,0:T(8,128)} %param.10) | copy-start | bytes 294916
  111.6 66.2 %copy-start.5 = (f32[1,48,512]{2,1,0:T(8,128)S(1)}, f32[1,48,512]{2,1,0:T(8,128)}, u32[]{:S(2)}) copy-start(f32[1,48,512]{2,1,0:T(8,128)} %param.9) | copy-start | bytes 294916
  173.1 3.5 %copy-start.1 = (bf16[2304,512]{1,0:T(8,128)(2,1)S(1)}, bf16[2304,512]{1,0:T(8,128)(2,1)}, u32[]{:S(2)}) copy-start(bf16[2304,512]{1,0:T(8,128)(2,1)} %all-gather.2.cloned.1.call-done) | copy-start | bytes 7077892
  178.7 8.1 %collective-permute-start = (bf16[48,512]{1,0:T(8,128)(2,1)S(1)}, bf16[48,512]{1,0:T(8,128)(2,1)S(1)}, u32[]{:S(2)}, u32[]{:S(2)}) collective-permute-start(bf16[48,512]{1,0:T(8,128)(2,1)S(1)} %get-tuple-element.5), channel_id=1, source_target_pairs={{0,48},{48,96},{96,144},{144,192},{192,240},{240,288},{288,336},{3... | collective-permute-start | bytes 147464 | tf_op jit(solution)/shard_map/ppermute | solution.py:43
  183.3 7.2 %collective-permute-start.1 = (bf16[48,512]{1,0:T(8,128)(2,1)S(1)}, bf16[48,512]{1,0:T(8,128)(2,1)S(1)}, u32[]{:S(2)}, u32[]{:S(2)}) collective-permute-start(bf16[48,512]{1,0:T(8,128)(2,1)S(1)} %get-tuple-element.5), channel_id=1, source_target_pairs={{0,720},{48,0},{96,48},{144,96},{192,144},{240,192},{288,240},{336... | collective-permute-start | bytes 147464 | tf_op jit(solution)/shard_map/ppermute | solution.py:43
Sparse Core Ops, SparseCore 0:
  13.9 29.9 reduce-scatter.3
  47.1 64.3 reduce-scatter.5
  114.6 24.3 reduce-scatter.7
Sparse Core Ops, SparseCore 1:
  48.7 124.3 all-gather.1
where the time goes:
time: 200 us
  waiting for transfers between devices  160 us (80%)
  between operations  17.1 us (9%)
  starting transfers between devices  6.69 us (3%)
  matrix products  6.33 us (3%)
  other arithmetic  5.7 us (3%)
  local copies, waits for them, and re-layouts  4.72 us (2%)
    reduce_scatter x3, waiting for transfers between devices, own_block(): blocks = lax.psum_scatter(blocks, axes[k], scatter_dimension=0, tiled=True)  94.3 us
    all_gather x1, waiting for transfers between devices, local(): gathered = lax.all_gather(compute_weights, FSDP, axis=0, tiled=True)  61.5 us
    ppermute x2, starting transfers between devices, from_behind(): lax.ppermute(shard, axis, [(i, (i + by) % length) for i in range(length)])  6.53 us
  transfers between devices with their start and end apart: 6, of which 4 were waited for; matrix products, arithmetic and copies ran while one was open for 4% of the time, Pallas kernels for 0%

commit v1 on v0

v1 whole, which is shorter than its diff:
```python
import functools
import math

import jax
import jax.numpy as jnp
from jax import lax
from jax.experimental import pallas as pl
from jax.experimental.pallas import tpu as pltpu
from jax.sharding import Mesh
from jax.sharding import PartitionSpec as P

FSDP = ("z", "xh", "core")


beta_one = 0.9
beta_two = 0.95
learn_rate = 0.05
weight_decay = 0.1
epsilon = 1e-08
correct_one = 1.0 - beta_one**5
correct_two = 1.0 - beta_two**5

f32, bf16 = jnp.float32, jnp.bfloat16


def swap(shard, axis):
    return lax.ppermute(shard, axis, [(0, 1), (1, 0)])


def from_behind(shard, axis, by):
    length = lax.axis_size(axis)
    return lax.ppermute(shard, axis, [(i, (i + by) % length) for i in range(length)])


def kernel_call(body, ins, outs, flops, scratch=()):
    vmem, smem = pltpu.VMEM, pltpu.SMEM
    moved = sum(a.size * a.dtype.itemsize for a in (*ins, *outs))
    limit = moved + sum(math.prod(s.shape) * 2 for s in scratch) + (4 << 20)
    return pl.pallas_call(
        body,
        out_shape=outs,
        in_specs=[pl.BlockSpec(memory_space=smem if a.size < 8 else vmem) for a in ins],
        out_specs=[pl.BlockSpec(memory_space=vmem) for _ in outs],
        scratch_shapes=scratch,
        compiler_params=pltpu.CompilerParams(vmem_limit_bytes=limit),
        cost_estimate=pl.CostEstimate(flops=flops, bytes_accessed=moved, transcendentals=0),
    )(*ins)


def choose(flag, first, second):
    return jnp.where(flag == 0, first, second), jnp.where(flag == 0, second, first)


def terms_body(factor, place, activations, upstream, keep, give):
    chunk = 384
    pairs = chunk // (2 * 48)
    right = upstream[...]
    for i in range(activations.shape[1] // chunk):
        left = activations[:, i * chunk : (i + 1) * chunk]
        part = lax.dot_general(left, right, (((0,), (0,)), ((), ())), preferred_element_type=f32)
        part = (part * factor).reshape(pairs, 2, 48, right.shape[1])
        mine, theirs = choose(place[1], part[:, 0], part[:, 1])
        keep[i * pairs : (i + 1) * pairs] = mine
        give[i * pairs : (i + 1) * pairs] = theirs.astype(bf16)


def core_sum_body(place, keep, theirs, keep_x, give_x):
    for z in range(keep_x.shape[0]):
        low, high = (keep[2 * z + k] + theirs[2 * z + k].astype(f32) for k in (0, 1))
        mine, other = choose(place[0], low, high)
        keep_x[z] = mine
        give_x[z] = other.astype(bf16)


def x_sum_body(keep, theirs, terms):
    for z in range(keep.shape[0]):
        terms[z] = (keep[z] + theirs[z].astype(f32)).astype(bf16)


def adam_body(terms, master, one, two, one_out, two_out, stepped, stepped_low):
    for row in range(0, master.shape[0], 16):
        rows = slice(row, row + 16)
        gradient = terms[0, rows].astype(f32)
        for z in range(1, terms.shape[0]):
            gradient = gradient + terms[z, rows].astype(f32)
        first = beta_one * one[rows] + (1.0 - beta_one) * gradient
        second = beta_two * two[rows] + (1.0 - beta_two) * gradient * gradient
        one_out[rows] = first
        two_out[rows] = second
        update = first / correct_one / (jnp.sqrt(second / correct_two) + epsilon)
        value = master[rows] - learn_rate * (update + weight_decay * master[rows])
        stepped[rows] = value
        stepped_low[rows] = value.astype(bf16)


def use_body(factor, place, own, x, core, core_x, activations, upstream, key_out, input_grad, full):
    rows = own.shape[1]
    for piece, xh, c in (
        (own, place[0], place[1]),
        (x, 1 - place[0], place[1]),
        (core, place[0], 1 - place[1]),
        (core_x, 1 - place[0], 1 - place[1]),
    ):
        for z in range(own.shape[0]):
            start = pl.multiple_of(z * 4 * rows + (2 * xh + c) * rows, 16)
            full[pl.ds(start, rows), :] = piece[z]
    left = upstream[...]
    chunk = 256
    for i in range(full.shape[0] // chunk):
        part = lax.dot_general(
            left,
            full[i * chunk : (i + 1) * chunk, :],
            (((1,), (1,)), ((), ())),
            preferred_element_type=f32,
        )
        input_grad[:, i * chunk : (i + 1) * chunk] = (part * factor).astype(bf16)
    part = jnp.dot(activations[...], full[...], preferred_element_type=f32)
    key_out[...] = (part * factor).astype(bf16)


def local(tokens, cotangent, weights, moment_one, moment_two, gossip):
    activations = tokens[0]
    upstream = cotangent[0]
    factor = 1.0 / math.sqrt(activations.shape[1])
    place = jnp.stack([lax.axis_index("xh"), lax.axis_index("core")]).astype(jnp.int32)
    length = lax.axis_size("z")
    rows, keys = weights.shape[1:]
    flops = 2 * activations.size * keys
    block = lambda lead, dtype: jax.ShapeDtypeStruct((lead, rows, keys), dtype)
    flat = lambda dtype: jax.ShapeDtypeStruct((rows, keys), dtype)

    keep, give = kernel_call(
        functools.partial(terms_body, factor),
        (place, activations, upstream),
        (block(2 * length, f32), block(2 * length, bf16)),
        flops,
    )
    theirs = swap(give, "core")
    keep, give = kernel_call(
        core_sum_body, (place, keep, theirs), (block(length, f32), block(length, bf16)), keep.size
    )
    theirs = swap(give, "xh")

    compute_weights = weights[0].astype(bf16)
    column = lax.all_gather(compute_weights, "z", axis=0)
    column_x = swap(column, "xh")
    column_core = swap(column, "core")

    (terms,) = kernel_call(x_sum_body, (keep, theirs), (block(length, bf16),), keep.size)
    terms = lax.all_to_all(terms, "z", 0, 0, tiled=True)

    moment_one_out, moment_two_out, stepped, stepped_low = kernel_call(
        adam_body,
        (terms, weights[0], moment_one[0], moment_two[0]),
        (flat(f32), flat(f32), flat(f32), flat(bf16)),
        terms.size,
    )
    left_side = from_behind(stepped_low, "blk", 1).astype(f32)
    right_side = from_behind(stepped_low, "blk", -1).astype(f32)
    mix_weights = gossip[0].astype(f32)
    averaged = (
        mix_weights[0] * left_side + mix_weights[1] * stepped + mix_weights[2] * right_side
    ) / (mix_weights[0] + mix_weights[1] + mix_weights[2])

    column_core_x = swap(column_x, "core")
    key_out, input_grad = kernel_call(
        functools.partial(use_body, factor),
        (place, column, column_x, column_core, column_core_x, activations, upstream),
        (
            jax.ShapeDtypeStruct((activations.shape[0], keys), bf16),
            jax.ShapeDtypeStruct(activations.shape, bf16),
        ),
        2 * flops,
        (pltpu.VMEM((4 * length * rows, keys), bf16),),
    )
    return (
        key_out[None],
        input_grad[None],
        averaged[None],
        moment_one_out[None],
        moment_two_out[None],
    )


def solution(mesh):
    split = Mesh(mesh.devices.reshape(mesh.shape["blk"], 12, 2, 2), ("blk",) + FSDP)
    spec = P("blk", FSDP, None)

    return jax.shard_map(
        local,
        mesh=split,
        in_specs=(spec,) * 5 + (P("blk", None),),
        out_specs=(spec,) * 5,
        check_vma=False,
    )
```

time: 200 us -> 123 us (0.61)
  the two profiles are of different devices: /device:TPU:24 before, /device:TPU:1 now
where the time goes in v1:
time: 123 us
  starting transfers between devices  49.4 us (40%)
  blocking collectives  37.1 us (30%)
  waiting for transfers between devices  18.5 us (15%)
  Pallas kernels  6.42 us (5%)
  local copies, waits for them, and re-layouts  6.2 us (5%)
  between operations  2.69 us (2%)
  other arithmetic  2.63 us (2%)
    all_gather x1, blocking collectives, local(): column = lax.all_gather(compute_weights, 'z', axis=0)  37.1 us
    ppermute x5, starting transfers between devices, swap(): return lax.ppermute(shard, axis, [(0, 1), (1, 0)])  35.4 us
    ppermute x5, waiting for transfers between devices, swap(): return lax.ppermute(shard, axis, [(0, 1), (1, 0)])  18.4 us
    ppermute x2, starting transfers between devices, from_behind(): lax.ppermute(shard, axis, [(i, (i + by) % length) for i in range(length)])  7.93 us
    pallas_call x5, Pallas kernels, kernel_call(): pl.pallas_call(body, out_shape=outs, in_specs=[pl.BlockSpec(memory_space=...  6.42 us
    all_to_all x1, starting transfers between devices, local(): terms = lax.all_to_all(terms, 'z', 0, 0, tiled=True)  6.02 us
    unnamed x18, local copies, waits for them, and re-layouts  5.55 us
    broadcast_in_dim x1, other arithmetic, local(): averaged[None]  2.54 us
  transfers between devices with their start and end apart: 8, of which 2 were waited for; matrix products, arithmetic and copies ran while one was open for 1% of the time, Pallas kernels for 3%

profile of v1, /device:TPU:1, one launch (start us, length us, event | category | flops | bytes accessed | tf_op | source)
XLA Modules:
  0.0 122.8 jit_solution(4990905697555728314)
XLA Ops:
  0.7 1.1 copy-done
  1.8 0.9 copy-done.4
  2.7 1.3 %shard_map.102 = (f32[24,48,512]{2,1,0:T(8,128)S(1)}, bf16[24,48,512]{2,1,0:T(8,128)(2,1)S(1)}) custom-call(s32[2]{0:T(128)S(1)} %pad_add_fusion.place, bf16[128,2304]{1,0:T(8,128)(2,1)S(1)} %bitcast.16, bf16[128,512]{1,0:T(8,128)(2,1)S(1)} %bitcast.19), custom_call_target="tpu_custom_call" | custom-call | flops 301989888 | bytes 4259848 | tf_op jit(solution)/shard_map/pallas_call | solution.py:39
  4.0 12.4 %collective-permute-start.3 = (bf16[24,48,512]{2,1,0:T(8,128)(2,1)S(1)}, bf16[24,48,512]{2,1,0:T(8,128)(2,1)S(1)}, u32[]{:S(2)}, u32[]{:S(2)}) collective-permute-start(bf16[24,48,512]{2,1,0:T(8,128)(2,1)S(1)} %get-tuple-element.18), channel_id=1, source_target_pairs={{0,1},{1,0},{2,3},{3,2},{4,5},{5,4},{6,7},{7,6},{8,9},{9,8},{10,11... | collective-permute-start | bytes 3538952 | tf_op jit(solution)/shard_map/ppermute | solution.py:27
  16.4 2.5 %collective-permute-done.3.theirs = bf16[24,48,512]{2,1,0:T(8,128)(2,1)S(1)} collective-permute-done((bf16[24,48,512]{2,1,0:T(8,128)(2,1)S(1)}, bf16[24,48,512]{2,1,0:T(8,128)(2,1)S(1)}, u32[]{:S(2)}, u32[]{:S(2)}) %collective-permute-start.3) | collective-permute-done | bytes 1179680 | tf_op jit(solution)/shard_map/ppermute | solution.py:27
  18.9 0.8 shard_map.103
  19.7 1.9 %collective-permute-start.4 = (bf16[12,48,512]{2,1,0:T(8,128)(2,1)S(1)}, bf16[12,48,512]{2,1,0:T(8,128)(2,1)S(1)}, u32[]{:S(2)}, u32[]{:S(2)}) collective-permute-start(bf16[12,48,512]{2,1,0:T(8,128)(2,1)S(1)} %get-tuple-element.20), channel_id=1, source_target_pairs={{0,2},{2,0},{1,3},{3,1},{4,6},{6,4},{5,7},{7,5},{8,10},{10,8},{9,1... | collective-permute-start | bytes 1769480 | tf_op jit(solution)/shard_map/ppermute | solution.py:27
  21.6 16.0 %collective-permute-done.4.theirs = bf16[12,48,512]{2,1,0:T(8,128)(2,1)S(1)} collective-permute-done((bf16[12,48,512]{2,1,0:T(8,128)(2,1)S(1)}, bf16[12,48,512]{2,1,0:T(8,128)(2,1)S(1)}, u32[]{:S(2)}, u32[]{:S(2)}) %collective-permute-start.4) | collective-permute-done | bytes 589856 | tf_op jit(solution)/shard_map/ppermute | solution.py:27
  37.6 0.9 shard_map.104
  38.5 6.0 %all-to-all-start = ((bf16[12,48,512]{2,1,0:T(8,128)(2,1)}), bf16[12,48,512]{2,1,0:T(8,128)(2,1)S(1)}, u32[]{:S(2)}, u32[]{:S(2)}) async-start(bf16[12,48,512]{2,1,0:T(8,128)(2,1)} %shard_map.104), calls=%async_computation | async-start | bytes 1179648 | tf_op jit(solution)/shard_map/all_to_all | solution.py:150
  44.6 37.1 %all_gather.4.own = bf16[12,48,512]{2,1,0:T(8,128)(2,1)S(1)} all-gather(bf16[1,48,512]{2,1,0:T(8,128)(2,1)S(1)} %convert_element_type.14), channel_id=1, replica_groups=mesh['blk'=16,'z'=12,'xh'=2,'core'=2] {'z'}, dimensions={0}, use_global_device_ids=true | all-gather | bytes 638976 | tf_op jit(solution)/shard_map/all_gather | solution.py:145
  81.7 4.6 %collective-permute-start = (bf16[12,48,512]{2,1,0:T(8,128)(2,1)S(1)}, bf16[12,48,512]{2,1,0:T(8,128)(2,1)S(1)}, u32[]{:S(2)}, u32[]{:S(2)}) collective-permute-start(bf16[12,48,512]{2,1,0:T(8,128)(2,1)S(1)} %all_gather.4.own), channel_id=1, source_target_pairs={{0,2},{2,0},{1,3},{3,1},{4,6},{6,4},{5,7},{7,5},{8,10},{10,8},{9,1... | collective-permute-start | bytes 1769480 | tf_op jit(solution)/shard_map/ppermute | solution.py:27
  86.3 8.1 %collective-permute-start.1 = (bf16[12,48,512]{2,1,0:T(8,128)(2,1)S(1)}, bf16[12,48,512]{2,1,0:T(8,128)(2,1)S(1)}, u32[]{:S(2)}, u32[]{:S(2)}) collective-permute-start(bf16[12,48,512]{2,1,0:T(8,128)(2,1)S(1)} %all_gather.4.own), channel_id=1, source_target_pairs={{0,1},{1,0},{2,3},{3,2},{4,5},{5,4},{6,7},{7,6},{8,9},{9,8},{10,11... | collective-permute-start | bytes 1769480 | tf_op jit(solution)/shard_map/ppermute | solution.py:27
  94.5 8.3 %collective-permute-start.2 = (bf16[12,48,512]{2,1,0:T(8,128)(2,1)S(1)}, bf16[12,48,512]{2,1,0:T(8,128)(2,1)S(1)}, u32[]{:S(2)}, u32[]{:S(2)}) collective-permute-start(bf16[12,48,512]{2,1,0:T(8,128)(2,1)S(1)} %collective-permute-done.x), channel_id=1, source_target_pairs={{0,1},{1,0},{2,3},{3,2},{4,5},{5,4},{6,7},{7,6},{8,9},{9,8},{10,11... | collective-permute-start | bytes 1769480 | tf_op jit(solution)/shard_map/ppermute | solution.py:27
  102.8 0.6 fusion
  105.4 0.9 copy-done.3
  106.3 0.9 copy-done.6
  107.2 0.9 copy-done.7
  108.0 0.8 shard_map.105
  108.8 3.2 %collective-permute-start.5 = (bf16[48,512]{1,0:T(8,128)(2,1)S(1)}, bf16[48,512]{1,0:T(8,128)(2,1)S(1)}, u32[]{:S(2)}, u32[]{:S(2)}) collective-permute-start(bf16[48,512]{1,0:T(8,128)(2,1)S(1)} %get-tuple-element.21), channel_id=1, source_target_pairs={{0,48},{48,96},{96,144},{144,192},{192,240},{240,288},{288,336},{3... | collective-permute-start | bytes 147464 | tf_op jit(solution)/shard_map/ppermute | solution.py:32
  112.0 4.7 %collective-permute-start.6 = (bf16[48,512]{1,0:T(8,128)(2,1)S(1)}, bf16[48,512]{1,0:T(8,128)(2,1)S(1)}, u32[]{:S(2)}, u32[]{:S(2)}) collective-permute-start(bf16[48,512]{1,0:T(8,128)(2,1)S(1)} %get-tuple-element.21), channel_id=1, source_target_pairs={{0,720},{48,0},{96,48},{144,96},{192,144},{240,192},{288,240},{336... | collective-permute-start | bytes 147464 | tf_op jit(solution)/shard_map/ppermute | solution.py:32
  116.8 0.9 copy-done.5
  117.7 2.6 %shard_map.101 = (bf16[128,512]{1,0:T(8,128)(2,1)}, bf16[128,2304]{1,0:T(8,128)(2,1)}) custom-call(s32[2]{0:T(128)S(1)} %pad_add_fusion.place, bf16[12,48,512]{2,1,0:T(8,128)(2,1)S(1)} %all_gather.4.own, bf16[12,48,512]{2,1,0:T(8,128)(2,1)S(1)} %collective-permute-done.x, bf16[12,48,512]{2,1,0:T(8,128)(2,1)S(1)} %collective-permute-done.1.core, ...), custom_call_target="tpu_custom_call" | custom-call | flops 603979776 | bytes 3801096 | tf_op jit(solution)/shard_map/pallas_call | solution.py:39
  120.3 2.5 %divide_bitcast_fusion = f32[1,48,512]{2,1,0:T(8,128)} fusion(bf16[48,512]{1,0:T(8,128)(2,1)S(1)} %collective-permute-done.6, f32[48,512]{1,0:T(8,128)S(1)} %get-tuple-element.22, bf16[48,512]{1,0:T(8,128)(2,1)S(1)} %collective-permute-done.5, f32[]{:T(128)S(6)} %add.15, f32[]{:T(128)} %bitcast.11, f32[]{:T(128)} %bitcast.10, f32[]{:T(128)} %bitcast.6), kind=kLoop, calls=%fused_computation | loop fusion | flops 196608 | bytes 294928 | tf_op jit(solution)/shard_map/broadcast_in_dim | solution.py:179
  (21 shorter events, 0.1 us)
Async XLA Ops:
  0.7 1.1 copy-start
  1.8 0.9 copy-start.4
  4.0 14.8 %collective-permute-start.3 = (bf16[24,48,512]{2,1,0:T(8,128)(2,1)S(1)}, bf16[24,48,512]{2,1,0:T(8,128)(2,1)S(1)}, u32[]{:S(2)}, u32[]{:S(2)}) collective-permute-start(bf16[24,48,512]{2,1,0:T(8,128)(2,1)S(1)} %get-tuple-element.18), channel_id=1, source_target_pairs={{0,1},{1,0},{2,3},{3,2},{4,5},{5,4},{6,7},{7,6},{8,9},{9,8},{10,11... | collective-permute-start | bytes 3538952 | tf_op jit(solution)/shard_map/ppermute | solution.py:27
  19.7 17.9 %collective-permute-start.4 = (bf16[12,48,512]{2,1,0:T(8,128)(2,1)S(1)}, bf16[12,48,512]{2,1,0:T(8,128)(2,1)S(1)}, u32[]{:S(2)}, u32[]{:S(2)}) collective-permute-start(bf16[12,48,512]{2,1,0:T(8,128)(2,1)S(1)} %get-tuple-element.20), channel_id=1, source_target_pairs={{0,2},{2,0},{1,3},{3,1},{4,6},{6,4},{5,7},{7,5},{8,10},{10,8},{9,1... | collective-permute-start | bytes 1769480 | tf_op jit(solution)/shard_map/ppermute | solution.py:27
  38.5 6.0 %copy-start.2 = (f32[1,48,512]{2,1,0:T(8,128)S(1)}, f32[1,48,512]{2,1,0:T(8,128)}, u32[]{:S(2)}) copy-start(f32[1,48,512]{2,1,0:T(8,128)} %param.8) | copy-start | bytes 294916
  38.5 64.3 %copy-start.8 = (s32[1,3]{1,0:T(1,128)S(1)}, s32[1,3]{1,0:T(1,128)}, u32[]{:S(2)}) copy-start(s32[1,3]{1,0:T(1,128)} %param.11) | copy-start | bytes 40
  38.5 78.3 %copy-start.1 = (bf16[1,128,2304]{2,1,0:T(8,128)(2,1)S(1)}, bf16[1,128,2304]{2,1,0:T(8,128)(2,1)}, u32[]{:S(2)}) copy-start(bf16[1,128,2304]{2,1,0:T(8,128)(2,1)} %param.6) | copy-start | bytes 1769476
  38.5 66.8 %all-to-all-start = ((bf16[12,48,512]{2,1,0:T(8,128)(2,1)}), bf16[12,48,512]{2,1,0:T(8,128)(2,1)S(1)}, u32[]{:S(2)}, u32[]{:S(2)}) async-start(bf16[12,48,512]{2,1,0:T(8,128)(2,1)} %shard_map.104), calls=%async_computation | async-start | bytes 1179648 | tf_op jit(solution)/shard_map/all_to_all | solution.py:150
  81.7 12.8 %collective-permute-start = (bf16[12,48,512]{2,1,0:T(8,128)(2,1)S(1)}, bf16[12,48,512]{2,1,0:T(8,128)(2,1)S(1)}, u32[]{:S(2)}, u32[]{:S(2)}) collective-permute-start(bf16[12,48,512]{2,1,0:T(8,128)(2,1)S(1)} %all_gather.4.own), channel_id=1, source_target_pairs={{0,2},{2,0},{1,3},{3,1},{4,6},{6,4},{5,7},{7,5},{8,10},{10,8},{9,1... | collective-permute-start | bytes 1769480 | tf_op jit(solution)/shard_map/ppermute | solution.py:27
  86.3 30.5 %collective-permute-start.1 = (bf16[12,48,512]{2,1,0:T(8,128)(2,1)S(1)}, bf16[12,48,512]{2,1,0:T(8,128)(2,1)S(1)}, u32[]{:S(2)}, u32[]{:S(2)}) collective-permute-start(bf16[12,48,512]{2,1,0:T(8,128)(2,1)S(1)} %all_gather.4.own), channel_id=1, source_target_pairs={{0,1},{1,0},{2,3},{3,2},{4,5},{5,4},{6,7},{7,6},{8,9},{9,8},{10,11... | collective-permute-start | bytes 1769480 | tf_op jit(solution)/shard_map/ppermute | solution.py:27
  94.5 22.3 %collective-permute-start.2 = (bf16[12,48,512]{2,1,0:T(8,128)(2,1)S(1)}, bf16[12,48,512]{2,1,0:T(8,128)(2,1)S(1)}, u32[]{:S(2)}, u32[]{:S(2)}) collective-permute-start(bf16[12,48,512]{2,1,0:T(8,128)(2,1)S(1)} %collective-permute-done.x), channel_id=1, source_target_pairs={{0,1},{1,0},{2,3},{3,2},{4,5},{5,4},{6,7},{7,6},{8,9},{9,8},{10,11... | collective-permute-start | bytes 1769480 | tf_op jit(solution)/shard_map/ppermute | solution.py:27
  105.4 0.9 copy-start.3
  106.3 0.9 copy-start.6
  107.2 0.9 copy-start.7
  108.8 11.4 %collective-permute-start.5 = (bf16[48,512]{1,0:T(8,128)(2,1)S(1)}, bf16[48,512]{1,0:T(8,128)(2,1)S(1)}, u32[]{:S(2)}, u32[]{:S(2)}) collective-permute-start(bf16[48,512]{1,0:T(8,128)(2,1)S(1)} %get-tuple-element.21), channel_id=1, source_target_pairs={{0,48},{48,96},{96,144},{144,192},{192,240},{240,288},{288,336},{3... | collective-permute-start | bytes 147464 | tf_op jit(solution)/shard_map/ppermute | solution.py:32
  112.0 8.2 %collective-permute-start.6 = (bf16[48,512]{1,0:T(8,128)(2,1)S(1)}, bf16[48,512]{1,0:T(8,128)(2,1)S(1)}, u32[]{:S(2)}, u32[]{:S(2)}) collective-permute-start(bf16[48,512]{1,0:T(8,128)(2,1)S(1)} %get-tuple-element.21), channel_id=1, source_target_pairs={{0,720},{48,0},{96,48},{144,96},{192,144},{240,192},{288,240},{336... | collective-permute-start | bytes 147464 | tf_op jit(solution)/shard_map/ppermute | solution.py:32
  116.8 0.9 copy-start.5

commit v2 on v1

--- a/solution.py
+++ b/solution.py
@@ -102,7 +102,7 @@
         (core_x, 1 - place[0], 1 - place[1]),
     ):
         for z in range(own.shape[0]):
-            start = pl.multiple_of(z * 4 * rows + (2 * xh + c) * rows, 16)
+            start = pl.multiple_of((4 * z + 2 * xh + c) * rows, 16)
             full[pl.ds(start, rows), :] = piece[z]
     left = upstream[...]
     chunk = 256
@@ -118,11 +118,18 @@
     key_out[...] = (part * factor).astype(bf16)
 
 
+def mix_body(gossip, left, own, right, out):
+    before, self_, after = (gossip[0, k].astype(f32) for k in range(3))
+    total = before + self_ + after
+    value = before * left[...].astype(f32) + self_ * own[...] + after * right[...].astype(f32)
+    out[...] = value / total
+
+
 def local(tokens, cotangent, weights, moment_one, moment_two, gossip):
     activations = tokens[0]
     upstream = cotangent[0]
     factor = 1.0 / math.sqrt(activations.shape[1])
-    place = jnp.stack([lax.axis_index("xh"), lax.axis_index("core")]).astype(jnp.int32)
+    place = jnp.stack([lax.axis_index(a) for a in ("xh", "core")]).astype(jnp.int32)
     length = lax.axis_size("z")
     rows, keys = weights.shape[1:]
     flops = 2 * activations.size * keys
@@ -155,12 +162,11 @@
         (flat(f32), flat(f32), flat(f32), flat(bf16)),
         terms.size,
     )
-    left_side = from_behind(stepped_low, "blk", 1).astype(f32)
-    right_side = from_behind(stepped_low, "blk", -1).astype(f32)
-    mix_weights = gossip[0].astype(f32)
-    averaged = (
-        mix_weights[0] * left_side + mix_weights[1] * stepped + mix_weights[2] * right_side
-    ) / (mix_weights[0] + mix_weights[1] + mix_weights[2])
+    left_side = from_behind(stepped_low, "blk", 1)
+    right_side = from_behind(stepped_low, "blk", -1)
+    (averaged,) = kernel_call(
+        mix_body, (gossip, left_side, stepped, right_side), (flat(f32),), 5 * stepped.size
+    )
 
     column_core_x = swap(column_x, "core")
     key_out, input_grad = kernel_call(

time: 123 us -> 120 us (0.976)
  other arithmetic: 2.63 us -> 0.08 us
  between operations: 2.69 us -> 0.81 us
    broadcast_in_dim x1 -> x0, other arithmetic: 2.54 us -> none  [local(): averaged[None]]
    pallas_call x5 -> x6, Pallas kernels: 6.42 us -> 7.63 us  [kernel_call(): pl.pallas_call(body, out_shape=outs, in_specs=[pl.BlockSpec(memory_space=...]
  transfers between devices with their start and end apart: 8 -> 8, of which waited for: 2 -> 2; matrix products, arithmetic and copies ran while one was open for 1% -> 0% of each run, Pallas kernels for 3% -> 3%
where the time goes in v2:
time: 120 us; the launch traced here: 119 us
  starting transfers between devices  49.5 us (41%)
  blocking collectives  37.1 us (31%)
  waiting for transfers between devices  18.5 us (15%)
  Pallas kernels  7.63 us (6%)
  local copies, waits for them, and re-layouts  5.55 us (5%)
    all_gather x1, blocking collectives, local(): column = lax.all_gather(compute_weights, 'z', axis=0)  37.1 us
    ppermute x5, starting transfers between devices, swap(): return lax.ppermute(shard, axis, [(0, 1), (1, 0)])  35.4 us
    ppermute x5, waiting for transfers between devices, swap(): return lax.ppermute(shard, axis, [(0, 1), (1, 0)])  18.4 us
    ppermute x2, starting transfers between devices, from_behind(): lax.ppermute(shard, axis, [(i, (i + by) % length) for i in range(length)])  8.06 us
    pallas_call x6, Pallas kernels, kernel_call(): pl.pallas_call(body, out_shape=outs, in_specs=[pl.BlockSpec(memory_space=...  7.63 us
    all_to_all x1, starting transfers between devices, local(): terms = lax.all_to_all(terms, 'z', 0, 0, tiled=True)  6.02 us
    unnamed x18, local copies, waits for them, and re-layouts  5.55 us
  transfers between devices with their start and end apart: 8, of which 2 were waited for; matrix products, arithmetic and copies ran while one was open for 0% of the time, Pallas kernels for 3%

profile of v2, /device:TPU:1, one launch (start us, length us, event | category | flops | bytes accessed | tf_op | source)
XLA Modules:
  0.0 119.1 jit_solution(5394888969433723345)
XLA Ops:
  0.6 0.1 pad_add_fusion.place
  0.7 1.1 copy-done
  1.8 0.9 copy-done.4
  2.7 1.3 %shard_map.102 = (f32[24,48,512]{2,1,0:T(8,128)S(1)}, bf16[24,48,512]{2,1,0:T(8,128)(2,1)S(1)}) custom-call(s32[2]{0:T(128)S(1)} %pad_add_fusion.place, bf16[128,2304]{1,0:T(8,128)(2,1)S(1)} %bitcast.12, bf16[128,512]{1,0:T(8,128)(2,1)S(1)} %bitcast.15), custom_call_target="tpu_custom_call" | custom-call | flops 301989888 | bytes 4259848 | tf_op jit(solution)/shard_map/pallas_call | solution.py:39
  4.0 12.4 %collective-permute-start.3 = (bf16[24,48,512]{2,1,0:T(8,128)(2,1)S(1)}, bf16[24,48,512]{2,1,0:T(8,128)(2,1)S(1)}, u32[]{:S(2)}, u32[]{:S(2)}) collective-permute-start(bf16[24,48,512]{2,1,0:T(8,128)(2,1)S(1)} %get-tuple-element.18), channel_id=1, source_target_pairs={{0,1},{1,0},{2,3},{3,2},{4,5},{5,4},{6,7},{7,6},{8,9},{9,8},{10,11... | collective-permute-start | bytes 3538952 | tf_op jit(solution)/shard_map/ppermute | solution.py:27
  16.4 2.5 %collective-permute-done.3.theirs = bf16[24,48,512]{2,1,0:T(8,128)(2,1)S(1)} collective-permute-done((bf16[24,48,512]{2,1,0:T(8,128)(2,1)S(1)}, bf16[24,48,512]{2,1,0:T(8,128)(2,1)S(1)}, u32[]{:S(2)}, u32[]{:S(2)}) %collective-permute-start.3) | collective-permute-done | bytes 1179680 | tf_op jit(solution)/shard_map/ppermute | solution.py:27
  18.9 0.8 shard_map.103
  19.7 1.9 %collective-permute-start.4 = (bf16[12,48,512]{2,1,0:T(8,128)(2,1)S(1)}, bf16[12,48,512]{2,1,0:T(8,128)(2,1)S(1)}, u32[]{:S(2)}, u32[]{:S(2)}) collective-permute-start(bf16[12,48,512]{2,1,0:T(8,128)(2,1)S(1)} %get-tuple-element.20), channel_id=1, source_target_pairs={{0,2},{2,0},{1,3},{3,1},{4,6},{6,4},{5,7},{7,5},{8,10},{10,8},{9,1... | collective-permute-start | bytes 1769480 | tf_op jit(solution)/shard_map/ppermute | solution.py:27
  21.6 16.0 %collective-permute-done.4.theirs = bf16[12,48,512]{2,1,0:T(8,128)(2,1)S(1)} collective-permute-done((bf16[12,48,512]{2,1,0:T(8,128)(2,1)S(1)}, bf16[12,48,512]{2,1,0:T(8,128)(2,1)S(1)}, u32[]{:S(2)}, u32[]{:S(2)}) %collective-permute-start.4) | collective-permute-done | bytes 589856 | tf_op jit(solution)/shard_map/ppermute | solution.py:27
  37.6 0.9 shard_map.104
  38.5 6.0 %all-to-all-start = ((bf16[12,48,512]{2,1,0:T(8,128)(2,1)}), bf16[12,48,512]{2,1,0:T(8,128)(2,1)S(1)}, u32[]{:S(2)}, u32[]{:S(2)}) async-start(bf16[12,48,512]{2,1,0:T(8,128)(2,1)} %shard_map.104), calls=%async_computation | async-start | bytes 1179648 | tf_op jit(solution)/shard_map/all_to_all | solution.py:157
  44.6 37.1 %all_gather.4.own = bf16[12,48,512]{2,1,0:T(8,128)(2,1)S(1)} all-gather(bf16[1,48,512]{2,1,0:T(8,128)(2,1)S(1)} %convert_element_type.4), channel_id=1, replica_groups=mesh['blk'=16,'z'=12,'xh'=2,'core'=2] {'z'}, dimensions={0}, use_global_device_ids=true | all-gather | bytes 638976 | tf_op jit(solution)/shard_map/all_gather | solution.py:152
  81.7 4.6 %collective-permute-start = (bf16[12,48,512]{2,1,0:T(8,128)(2,1)S(1)}, bf16[12,48,512]{2,1,0:T(8,128)(2,1)S(1)}, u32[]{:S(2)}, u32[]{:S(2)}) collective-permute-start(bf16[12,48,512]{2,1,0:T(8,128)(2,1)S(1)} %all_gather.4.own), channel_id=1, source_target_pairs={{0,2},{2,0},{1,3},{3,1},{4,6},{6,4},{5,7},{7,5},{8,10},{10,8},{9,1... | collective-permute-start | bytes 1769480 | tf_op jit(solution)/shard_map/ppermute | solution.py:27
  86.3 8.1 %collective-permute-start.1 = (bf16[12,48,512]{2,1,0:T(8,128)(2,1)S(1)}, bf16[12,48,512]{2,1,0:T(8,128)(2,1)S(1)}, u32[]{:S(2)}, u32[]{:S(2)}) collective-permute-start(bf16[12,48,512]{2,1,0:T(8,128)(2,1)S(1)} %all_gather.4.own), channel_id=1, source_target_pairs={{0,1},{1,0},{2,3},{3,2},{4,5},{5,4},{6,7},{7,6},{8,9},{9,8},{10,11... | collective-permute-start | bytes 1769480 | tf_op jit(solution)/shard_map/ppermute | solution.py:27
  94.5 8.3 %collective-permute-start.2 = (bf16[12,48,512]{2,1,0:T(8,128)(2,1)S(1)}, bf16[12,48,512]{2,1,0:T(8,128)(2,1)S(1)}, u32[]{:S(2)}, u32[]{:S(2)}) collective-permute-start(bf16[12,48,512]{2,1,0:T(8,128)(2,1)S(1)} %collective-permute-done.x), channel_id=1, source_target_pairs={{0,1},{1,0},{2,3},{3,2},{4,5},{5,4},{6,7},{7,6},{8,9},{9,8},{10,11... | collective-permute-start | bytes 1769480 | tf_op jit(solution)/shard_map/ppermute | solution.py:27
  102.8 0.9 copy-done.3
  103.7 0.9 copy-done.6
  104.6 0.9 copy-done.7
  105.5 0.8 shard_map.105
  106.3 3.3 %collective-permute-start.5 = (bf16[48,512]{1,0:T(8,128)(2,1)S(1)}, bf16[48,512]{1,0:T(8,128)(2,1)S(1)}, u32[]{:S(2)}, u32[]{:S(2)}) collective-permute-start(bf16[48,512]{1,0:T(8,128)(2,1)S(1)} %get-tuple-element.21), channel_id=1, source_target_pairs={{0,48},{48,96},{96,144},{144,192},{192,240},{240,288},{288,336},{3... | collective-permute-start | bytes 147464 | tf_op jit(solution)/shard_map/ppermute | solution.py:32
  109.6 4.7 %collective-permute-start.6 = (bf16[48,512]{1,0:T(8,128)(2,1)S(1)}, bf16[48,512]{1,0:T(8,128)(2,1)S(1)}, u32[]{:S(2)}, u32[]{:S(2)}) collective-permute-start(bf16[48,512]{1,0:T(8,128)(2,1)S(1)} %get-tuple-element.21), channel_id=1, source_target_pairs={{0,720},{48,0},{96,48},{144,96},{192,144},{240,192},{288,240},{336... | collective-permute-start | bytes 147464 | tf_op jit(solution)/shard_map/ppermute | solution.py:32
  114.4 0.9 copy-done.5
  115.3 2.6 %shard_map.101 = (bf16[128,512]{1,0:T(8,128)(2,1)}, bf16[128,2304]{1,0:T(8,128)(2,1)}) custom-call(s32[2]{0:T(128)S(1)} %pad_add_fusion.place, bf16[12,48,512]{2,1,0:T(8,128)(2,1)S(1)} %all_gather.4.own, bf16[12,48,512]{2,1,0:T(8,128)(2,1)S(1)} %collective-permute-done.x, bf16[12,48,512]{2,1,0:T(8,128)(2,1)S(1)} %collective-permute-done.1.core, ...), custom_call_target="tpu_custom_call" | custom-call | flops 603979776 | bytes 3801096 | tf_op jit(solution)/shard_map/pallas_call | solution.py:39
  117.9 1.2 %shard_map.106 = f32[48,512]{1,0:T(8,128)} custom-call(s32[1,3]{1,0:T(1,128)S(1)} %copy-done.8, bf16[48,512]{1,0:T(8,128)(2,1)S(1)} %collective-permute-done.5.left, f32[48,512]{1,0:T(8,128)S(1)} %get-tuple-element.22.own, bf16[48,512]{1,0:T(8,128)(2,1)S(1)} %collective-permute-done.6.right), custom_call_target="tpu_custom_call" | custom-call | flops 122880 | bytes 294924 | tf_op jit(solution)/shard_map/pallas_call | solution.py:39
  (19 shorter events, 0.1 us)
Async XLA Ops:
  0.7 1.1 copy-start
  1.8 0.9 copy-start.4
  4.0 14.8 %collective-permute-start.3 = (bf16[24,48,512]{2,1,0:T(8,128)(2,1)S(1)}, bf16[24,48,512]{2,1,0:T(8,128)(2,1)S(1)}, u32[]{:S(2)}, u32[]{:S(2)}) collective-permute-start(bf16[24,48,512]{2,1,0:T(8,128)(2,1)S(1)} %get-tuple-element.18), channel_id=1, source_target_pairs={{0,1},{1,0},{2,3},{3,2},{4,5},{5,4},{6,7},{7,6},{8,9},{9,8},{10,11... | collective-permute-start | bytes 3538952 | tf_op jit(solution)/shard_map/ppermute | solution.py:27
  19.7 17.9 %collective-permute-start.4 = (bf16[12,48,512]{2,1,0:T(8,128)(2,1)S(1)}, bf16[12,48,512]{2,1,0:T(8,128)(2,1)S(1)}, u32[]{:S(2)}, u32[]{:S(2)}) collective-permute-start(bf16[12,48,512]{2,1,0:T(8,128)(2,1)S(1)} %get-tuple-element.20), channel_id=1, source_target_pairs={{0,2},{2,0},{1,3},{3,1},{4,6},{6,4},{5,7},{7,5},{8,10},{10,8},{9,1... | collective-permute-start | bytes 1769480 | tf_op jit(solution)/shard_map/ppermute | solution.py:27
  38.5 6.0 %copy-start.2 = (f32[1,48,512]{2,1,0:T(8,128)S(1)}, f32[1,48,512]{2,1,0:T(8,128)}, u32[]{:S(2)}) copy-start(f32[1,48,512]{2,1,0:T(8,128)} %param.8) | copy-start | bytes 294916
  38.5 75.9 %copy-start.1 = (bf16[1,128,2304]{2,1,0:T(8,128)(2,1)S(1)}, bf16[1,128,2304]{2,1,0:T(8,128)(2,1)}, u32[]{:S(2)}) copy-start(bf16[1,128,2304]{2,1,0:T(8,128)(2,1)} %param.6) | copy-start | bytes 1769476
  38.5 64.3 %all-to-all-start = ((bf16[12,48,512]{2,1,0:T(8,128)(2,1)}), bf16[12,48,512]{2,1,0:T(8,128)(2,1)S(1)}, u32[]{:S(2)}, u32[]{:S(2)}) async-start(bf16[12,48,512]{2,1,0:T(8,128)(2,1)} %shard_map.104), calls=%async_computation | async-start | bytes 1179648 | tf_op jit(solution)/shard_map/all_to_all | solution.py:157
  81.7 12.8 %collective-permute-start = (bf16[12,48,512]{2,1,0:T(8,128)(2,1)S(1)}, bf16[12,48,512]{2,1,0:T(8,128)(2,1)S(1)}, u32[]{:S(2)}, u32[]{:S(2)}) collective-permute-start(bf16[12,48,512]{2,1,0:T(8,128)(2,1)S(1)} %all_gather.4.own), channel_id=1, source_target_pairs={{0,2},{2,0},{1,3},{3,1},{4,6},{6,4},{5,7},{7,5},{8,10},{10,8},{9,1... | collective-permute-start | bytes 1769480 | tf_op jit(solution)/shard_map/ppermute | solution.py:27
  86.3 28.0 %collective-permute-start.1 = (bf16[12,48,512]{2,1,0:T(8,128)(2,1)S(1)}, bf16[12,48,512]{2,1,0:T(8,128)(2,1)S(1)}, u32[]{:S(2)}, u32[]{:S(2)}) collective-permute-start(bf16[12,48,512]{2,1,0:T(8,128)(2,1)S(1)} %all_gather.4.own), channel_id=1, source_target_pairs={{0,1},{1,0},{2,3},{3,2},{4,5},{5,4},{6,7},{7,6},{8,9},{9,8},{10,11... | collective-permute-start | bytes 1769480 | tf_op jit(solution)/shard_map/ppermute | solution.py:27
  94.5 19.9 %collective-permute-start.2 = (bf16[12,48,512]{2,1,0:T(8,128)(2,1)S(1)}, bf16[12,48,512]{2,1,0:T(8,128)(2,1)S(1)}, u32[]{:S(2)}, u32[]{:S(2)}) collective-permute-start(bf16[12,48,512]{2,1,0:T(8,128)(2,1)S(1)} %collective-permute-done.x), channel_id=1, source_target_pairs={{0,1},{1,0},{2,3},{3,2},{4,5},{5,4},{6,7},{7,6},{8,9},{9,8},{10,11... | collective-permute-start | bytes 1769480 | tf_op jit(solution)/shard_map/ppermute | solution.py:27
  102.8 0.9 copy-start.3
  103.7 0.9 copy-start.6
  104.6 0.9 copy-start.7
  106.3 11.6 %copy-start.8 = (s32[1,3]{1,0:T(1,128)S(1)}, s32[1,3]{1,0:T(1,128)}, u32[]{:S(2)}) copy-start(s32[1,3]{1,0:T(1,128)} %gossip.1) | copy-start | bytes 40
  106.3 11.6 %collective-permute-start.5 = (bf16[48,512]{1,0:T(8,128)(2,1)S(1)}, bf16[48,512]{1,0:T(8,128)(2,1)S(1)}, u32[]{:S(2)}, u32[]{:S(2)}) collective-permute-start(bf16[48,512]{1,0:T(8,128)(2,1)S(1)} %get-tuple-element.21), channel_id=1, source_target_pairs={{0,48},{48,96},{96,144},{144,192},{192,240},{240,288},{288,336},{3... | collective-permute-start | bytes 147464 | tf_op jit(solution)/shard_map/ppermute | solution.py:32
  109.6 8.2 %collective-permute-start.6 = (bf16[48,512]{1,0:T(8,128)(2,1)S(1)}, bf16[48,512]{1,0:T(8,128)(2,1)S(1)}, u32[]{:S(2)}, u32[]{:S(2)}) collective-permute-start(bf16[48,512]{1,0:T(8,128)(2,1)S(1)} %get-tuple-element.21), channel_id=1, source_target_pairs={{0,720},{48,0},{96,48},{144,96},{192,144},{240,192},{288,240},{336... | collective-permute-start | bytes 147464 | tf_op jit(solution)/shard_map/ppermute | solution.py:32
  114.4 0.9 copy-start.5
